TPU v7x, 32 devices: a whole 2x2x4 slice. The times are simulated.
32 devices in a mesh: row: 8 (over y, x, core), col: 4 (over z).
Axes of the slice: x: 2, y: 2, z: 4, core: 2. Of those that a mesh axis runs over, the one named last changes fastest.
Arguments:
- temps: bfloat16 [12, 64, 16384], P(None, None, ('row', 'col')), may hold values from -6 to 6
- sensors: int32 [12, 512], replicated, may hold values from 0 to 16383
Outputs:
- corr: bfloat16 [512, 16384], P('col', 'row')
Inputs may be any that keep to these rules, and one draw needn't show every extreme that they name: `sensors`: each entry is a pixel index of its tier; candidates may repeat.
All inputs are finite; a program needn't handle non-finite values.
Results may differ from a plain program's by a relative error of at most 0.001.
Values may be sent and summed in bfloat16 or wider, within the bound.
A program may use at most 64 MiB of HBM per device.

v0:
```python
import jax
import jax.numpy as jnp
from jax import lax
from jax.sharding import PartitionSpec as P


def select_columns(fields, sensor_rows, first_pixel):
    width = fields.shape[2]
    offsets = sensor_rows - first_pixel
    pixel_ids = lax.broadcasted_iota(jnp.int32, (width, sensor_rows.shape[1]), 0)

    def one_tier(pair):
        tier_fields, tier_offsets = pair
        selector = (pixel_ids == tier_offsets[None, :]).astype(jnp.bfloat16)
        return jnp.dot(tier_fields, selector, preferred_element_type=jnp.float32)

    return lax.map(one_tier, (fields, offsets))


def body(temps, sensors):
    col_count = lax.axis_size("col")
    first_pixel = (lax.axis_index("row") * col_count + lax.axis_index("col")) * temps.shape[2]
    local_values = select_columns(temps, sensors, first_pixel)
    owned = lax.psum_scatter(
        local_values.astype(jnp.bfloat16), "col", scatter_dimension=2, tiled=True
    )
    readings = lax.psum(owned, "row").astype(jnp.float32).astype(jnp.bfloat16)
    scale_factor = 1.0 / jnp.sqrt(jnp.float32(temps.shape[0] * temps.shape[1]))
    summed = jnp.einsum(
        "tsc,tsp->cp",
        lax.all_gather(readings, "col", axis=2, tiled=True),
        temps,
        preferred_element_type=jnp.float32,
    )
    rounded = (summed * scale_factor).astype(jnp.bfloat16)
    return lax.all_to_all(rounded, "col", split_axis=0, concat_axis=1, tiled=True)


def solution(mesh):
    placed = (P(None, None, ("row", "col")), P())
    return jax.shard_map(
        body, mesh=mesh, in_specs=placed, out_specs=P("col", "row"), check_vma=False
    )
```

profile of v0, /device:TPU:0, one launch (start us, length us, event | category | flops | bytes accessed | tf_op | source)
XLA Modules:
  0.0 149.4 jit_solution(5405462871860880620)
XLA Ops:
  6.5 0.8 broadcast_subtract_fusion
  7.3 14.2 %while.11 = (s32[]{:T(128)}, bf16[12,64,512]{2,1,0:T(8,128)(2,1)S(1)}, bf16[12,64,512]{2,1,0:T(8,128)(2,1)}, s32[12,512]{1,0:T(8,128)S(1)}, s32[]{:T(128)}) while((s32[]{:T(128)}, bf16[12,64,512]{2,1,0:T(8,128)(2,1)S(1)}, bf16[12,64,512]{2,1,0:T(8,128)(2,1)}, s32[12,512]{1,0:T(8,128)S(1)}, s32[]{:T(128)}) %tuple.21), condition=%wide.region_1.2_spmd.clone, body=%wide.region_0.1_spmd.clone.sunk | while | flops 33816576 | bytes 203849 | solution.py:17
  7.3 1.2 fusion.14
  8.5 1.2 fusion.14
  9.7 1.2 fusion.14
  10.9 1.2 fusion.14
  12.1 1.2 fusion.14
  13.2 1.2 fusion.14
  14.4 1.2 fusion.14
  15.6 1.2 fusion.14
  16.8 1.2 fusion.14
  18.0 1.2 fusion.14
  19.2 1.2 fusion.14
  20.4 1.2 fusion.14
  21.5 2.0 %copy.5 = bf16[12,64,512]{1,0,2:T(8,128)(2,1)S(1)} copy(bf16[12,64,512]{2,1,0:T(8,128)(2,1)S(1)} %get-tuple-element.32) | data formatting | bytes 1572864
  23.5 2.0 %reshape.4 = bf16[512,768]{1,0:T(8,128)(2,1)} reshape(bf16[512,12,64]{2,1,0:T(8,128)(2,1)S(1)} %bitcast.28) | data formatting | bytes 1572864
  25.7 26.0 %reduce-scatter.4.cloned.1.call-done = bf16[128,768]{1,0:T(8,128)(2,1)} async-done(((bf16[512,768]{1,0:T(8,128)(2,1)}), bf16[128,768]{1,0:T(8,128)(2,1)}) %reduce-scatter.4.cloned.1.call-update) | async-done | bytes 196624
  51.7 1.3 reshape.5
  52.9 1.0 copy.6
  54.0 53.9 %all-reduce.2.cloned.1.call-done = bf16[12,64,128]{2,1,0:T(8,128)(2,1)} async-done(((bf16[12,64,128]{2,1,0:T(8,128)(2,1)}), bf16[12,64,128]{2,1,0:T(8,128)(2,1)}) %all-reduce.2.cloned.1.call-update) | async-done | bytes 196624 | tf_op jit(solution)/shard_map/psum | solution.py:27
  107.9 18.8 %all_gather.3 = bf16[12,64,512]{2,1,0:T(8,128)(2,1)S(1)} all-gather(bf16[12,64,128]{2,1,0:T(8,128)(2,1)} %all-reduce.2.cloned.1.call-done), channel_id=1, replica_groups=mesh['row'=8,'col'=4] {'col'}, dimensions={2}, use_global_device_ids=true | all-gather | bytes 983040 | tf_op jit(solution)/shard_map/all_gather | solution.py:31
  126.7 0.6 fusion.8
  127.3 14.4 %all_to_all.19 = bf16[4,128,512]{2,1,0:T(8,128)(2,1)S(1)} all-to-all(bf16[4,128,512]{2,1,0:T(8,128)(2,1)S(1)} %bitcast.31), channel_id=1, replica_groups=mesh['row'=8,'col'=4] {'col'}, dimensions={0} | all-to-all | bytes 1048576 | tf_op jit(solution)/shard_map/all_to_all | solution.py:36
  141.8 0.8 copy.7
  (19 shorter events, 0.2 us)
Async XLA Ops:
  6.5 45.1 %reduce-scatter.4.cloned.1.call-start = ((), (), s32[]{:S(2)}) async-start(), calls=%async_computation.3 | async-start | bytes 983040
  25.6 101.2 %copy-start = (bf16[12,64,512]{2,1,0:T(8,128)(2,1)S(1)}, bf16[12,64,512]{2,1,0:T(8,128)(2,1)}, u32[]{:S(2)}) copy-start(bf16[12,64,512]{2,1,0:T(8,128)(2,1)} %get-tuple-element.99) | copy-start | bytes 2359300
  25.6 82.3 %all-reduce.2.cloned.1.call-start = ((), (), s32[]{:S(2)}) async-start(), calls=%async_computation.2 | async-start | bytes 393216 | tf_op jit(solution)/shard_map/psum | solution.py:27
Sparse Core Ops, SparseCore 0:
  25.7 25.8 reduce-scatter.3
  54.7 53.1 all-reduce.1
where the time goes:
time: 150 us; the launch traced here: 149 us
  waiting for transfers between devices  80 us (53%)
  blocking collectives  33.2 us (22%)
  matrix products  14.5 us (10%)
  between operations  13.4 us (9%)
  local copies, waits for them, and re-layouts  7.3 us (5%)
    psum x1, waiting for transfers between devices, body(): readings = lax.psum(owned, 'row').astype(jnp.float32).astype(jnp.bfloat16)  53.9 us
    unnamed x3, waiting for transfers between devices  26 us
    all_gather x1, blocking collectives, body(): lax.all_gather(readings, 'col', axis=2, tiled=True)  18.8 us
    all_to_all x1, blocking collectives, body(): lax.all_to_all(rounded, 'col', split_axis=0, concat_axis=1, tiled=True)  14.4 us
    dot_general x12, matrix products, one_tier(): return jnp.dot(tier_fields, selector, preferred_element_type=jnp.float32)  13.9 us
    unnamed x6, local copies, waits for them, and re-layouts  6.33 us
  transfers between devices with their start and end apart: 2, of which 2 were waited for; matrix products, arithmetic and copies ran while one was open for 0% of the time, Pallas kernels for 0%

commit v1 on v0

--- a/solution.py
+++ b/solution.py
@@ -24,7 +24,9 @@
     owned = lax.psum_scatter(
         local_values.astype(jnp.bfloat16), "col", scatter_dimension=2, tiled=True
     )
-    readings = lax.psum(owned, "row").astype(jnp.float32).astype(jnp.bfloat16)
+    readings = (
+        jnp.sum(lax.all_gather(owned, "row"), axis=0).astype(jnp.float32).astype(jnp.bfloat16)
+    )
     scale_factor = 1.0 / jnp.sqrt(jnp.float32(temps.shape[0] * temps.shape[1]))
     summed = jnp.einsum(
         "tsc,tsp->cp",

time: 150 us -> 125 us (0.83)
  waiting for transfers between devices: 80 us -> 51.2 us
  blocking collectives: 33.2 us -> 35.3 us
  other arithmetic: 0.76 us -> 2.45 us
    psum x1 -> x0, waiting for transfers between devices: 53.9 us -> none  [body(): readings = lax.psum(owned, 'row').astype(jnp.float32).astype(jnp.bfloat16)]
    all_gather x0 -> x1, waiting for transfers between devices: none -> 25.2 us  [body(): lax.all_gather(owned, 'row')]
    all_to_all x1, blocking collectives: 14.4 us -> 16.7 us  [body(): lax.all_to_all(rounded, 'col', split_axis=0, concat_axis=1, tiled=True)]
    reduce_sum x0 -> x1, other arithmetic: none -> 1.69 us  [body(): jnp.sum(lax.all_gather(owned, 'row'), axis=0).astype(jnp.float32)]
where the time goes in v1:
time: 125 us; the launch traced here: 124 us
  waiting for transfers between devices  51.2 us (41%)
  blocking collectives  35.3 us (28%)
  matrix products  14.5 us (12%)
  between operations  13.4 us (11%)
  local copies, waits for them, and re-layouts  7.3 us (6%)
  other arithmetic  2.45 us (2%)
    unnamed x3, waiting for transfers between devices  26 us
    all_gather x1, waiting for transfers between devices, body(): lax.all_gather(owned, 'row')  25.2 us
    all_gather x1, blocking collectives, body(): lax.all_gather(readings, 'col', axis=2, tiled=True)  18.6 us
    all_to_all x1, blocking collectives, body(): lax.all_to_all(rounded, 'col', split_axis=0, concat_axis=1, tiled=True)  16.7 us
    dot_general x12, matrix products, one_tier(): return jnp.dot(tier_fields, selector, preferred_element_type=jnp.float32)  13.9 us
    unnamed x6, local copies, waits for them, and re-layouts  6.34 us
  transfers between devices with their start and end apart: 2, of which 2 were waited for; matrix products, arithmetic and copies ran while one was open for 0% of the time, Pallas kernels for 0%

profile of v1, /device:TPU:0, one launch (start us, length us, event | category | flops | bytes accessed | tf_op | source)
XLA Modules:
  0.0 124.5 jit_solution(3413883939913348037)
XLA Ops:
  6.5 0.8 broadcast_subtract_fusion
  7.3 14.2 %while.11 = (s32[]{:T(128)}, bf16[12,64,512]{2,1,0:T(8,128)(2,1)S(1)}, bf16[12,64,512]{2,1,0:T(8,128)(2,1)}, s32[12,512]{1,0:T(8,128)S(1)}, s32[]{:T(128)}) while((s32[]{:T(128)}, bf16[12,64,512]{2,1,0:T(8,128)(2,1)S(1)}, bf16[12,64,512]{2,1,0:T(8,128)(2,1)}, s32[12,512]{1,0:T(8,128)S(1)}, s32[]{:T(128)}) %tuple.21), condition=%wide.region_1.2_spmd.clone, body=%wide.region_0.1_spmd.clone.sunk | while | flops 33816576 | bytes 203849 | solution.py:17
  7.3 1.2 fusion.14
  8.5 1.2 fusion.14
  9.7 1.2 fusion.14
  10.9 1.2 fusion.14
  12.1 1.2 fusion.14
  13.2 1.2 fusion.14
  14.4 1.2 fusion.14
  15.6 1.2 fusion.14
  16.8 1.2 fusion.14
  18.0 1.2 fusion.14
  19.2 1.2 fusion.14
  20.4 1.2 fusion.14
  21.5 2.0 %copy.5 = bf16[12,64,512]{1,0,2:T(8,128)(2,1)S(1)} copy(bf16[12,64,512]{2,1,0:T(8,128)(2,1)S(1)} %get-tuple-element.32) | data formatting | bytes 1572864
  23.5 2.0 %reshape.5 = bf16[512,768]{1,0:T(8,128)(2,1)} reshape(bf16[512,12,64]{2,1,0:T(8,128)(2,1)S(1)} %bitcast.29) | data formatting | bytes 1572864
  25.7 26.0 %reduce-scatter.4.cloned.1.call-done = bf16[128,768]{1,0:T(8,128)(2,1)} async-done(((bf16[512,768]{1,0:T(8,128)(2,1)}), bf16[128,768]{1,0:T(8,128)(2,1)}) %reduce-scatter.4.cloned.1.call-update) | async-done | bytes 196624
  51.7 1.3 %reshape.6 = bf16[128,12,64]{2,1,0:T(8,128)(2,1)S(1)} reshape(bf16[128,768]{1,0:T(8,128)(2,1)} %reduce-scatter.4.cloned.1.call-done) | data formatting | bytes 393216
  52.9 1.0 copy.6
  54.0 25.2 %all-gather.3.cloned.1.call-done = bf16[96,64,128]{2,1,0:T(8,128)(2,1)} async-done(((bf16[12,64,128]{2,1,0:T(8,128)(2,1)}), bf16[96,64,128]{2,1,0:T(8,128)(2,1)}) %all-gather.3.cloned.1.call-update) | async-done | bytes 1572880 | tf_op jit(solution)/shard_map/all_gather | solution.py:28
  79.2 1.7 %reduce_sum.12 = bf16[12,64,128]{2,1,0:T(8,128)(2,1)S(1)} reduce(bf16[8,12,64,128]{3,2,1,0:T(8,128)(2,1)} %bitcast.32, bf16[]{:T(256)} %constant.31.clone.1), dimensions={0}, to_apply=%region_3.4 | reduce | flops 688128 | bytes 1769474 | tf_op jit(solution)/shard_map/reduce_sum | solution.py:28
  80.9 18.6 %all_gather.11 = bf16[12,64,512]{2,1,0:T(8,128)(2,1)S(1)} all-gather(bf16[12,64,128]{2,1,0:T(8,128)(2,1)S(1)} %reduce_sum.12), channel_id=1, replica_groups=mesh['row'=8,'col'=4] {'col'}, dimensions={2}, use_global_device_ids=true | all-gather | bytes 983040 | tf_op jit(solution)/shard_map/all_gather | solution.py:33
  100.1 16.7 %all_to_all.19 = bf16[4,128,512]{2,1,0:T(8,128)(2,1)S(1)} all-to-all(bf16[4,128,512]{2,1,0:T(8,128)(2,1)S(1)} %bitcast.33), channel_id=1, replica_groups=mesh['row'=8,'col'=4] {'col'}, dimensions={0} | all-to-all | bytes 1048576 | tf_op jit(solution)/shard_map/all_to_all | solution.py:38
  116.8 0.8 copy.7
  (20 shorter events, 0.8 us)
Async XLA Ops:
  6.5 45.1 %reduce-scatter.4.cloned.1.call-start = ((), (), s32[]{:S(2)}) async-start(), calls=%async_computation.3 | async-start | bytes 983040
  25.6 73.9 %copy-start = (bf16[12,64,512]{2,1,0:T(8,128)(2,1)S(1)}, bf16[12,64,512]{2,1,0:T(8,128)(2,1)}, u32[]{:S(2)}) copy-start(bf16[12,64,512]{2,1,0:T(8,128)(2,1)} %get-tuple-element.99) | copy-start | bytes 2359300
  25.6 53.6 %all-gather.3.cloned.1.call-start = ((), (), s32[]{:S(2)}) async-start(), calls=%async_computation.2 | async-start | bytes 1769472 | tf_op jit(solution)/shard_map/all_gather | solution.py:28
Sparse Core Ops, SparseCore 0:
  25.7 25.8 reduce-scatter.3
  54.1 25.0 all-gather.2
